TPU v7x, 32 devices: a whole 2x2x4 slice. The times are simulated.
32 devices in a mesh: req: 2 (over y), blk: 4 (over z), uly: 4 (over x, core).
Axes of the slice: x: 2, y: 2, z: 4, core: 2. Of those that a mesh axis runs over, the one named last changes fastest.
Arguments:
- video_qkv: bfloat16 [3, 2048, 3072], P(None, ('req', 'blk', 'uly')), parts along dimension 1, may hold values from -16 to 16
- text_qkv: bfloat16 [3, 64, 3072], P(None, ('req', 'blk', 'uly')), parts along dimension 1, may hold values from -9.5625 to 9.5625
- video_gate: float32 [6144], P('req'), parts along dimension 0, may hold values from 1 to 4
- text_gate: float32 [6144], P('req'), parts along dimension 0, may hold values from 1 to 4
Outputs:
- video_out: bfloat16 [2048, 3072], P(('req', 'blk', 'uly')), parts along dimension 0
- text_out: bfloat16 [64, 3072], P(('req', 'blk', 'uly')), parts along dimension 0
There are 2 independent parts, one for each index of `req`. A program takes and returns all parts, laid end to end along the dimension named above; each array names one. Nothing has to cross between parts.
All inputs are finite; a program needn't handle non-finite values.
Results may differ from a plain program's by a relative error of at most 0.0085.
Values may be sent and summed in bfloat16 or wider, within the bound.
No kernel may reach another device: no remote copies, remote signals or barrier semaphores. Data moves between devices by JAX's collectives and lax.ppermute only.
A program may use at most 128 MiB of HBM per device.

v0:
```python
import math
import jax
import jax.numpy as jnp
from jax import lax
from jax.sharding import PartitionSpec as P

HEADS = 24
HD = 128


def merge_block(state, queries, block_pair):
    best, total, summed = state
    scale = 1.0 / math.sqrt(queries.shape[-1])
    scores = (
        jnp.einsum("qhd,khd->hqk", queries, block_pair[0], preferred_element_type=jnp.float32)
        * scale
    )
    new_best = jnp.maximum(best, jnp.max(scores, axis=2))
    factor = jnp.exp(best - new_best)
    raised = jnp.exp(scores - new_best[:, :, None])
    total = total * factor + jnp.sum(raised, axis=2)
    product = jnp.einsum(
        "hqk,khd->hqd",
        raised.astype(jnp.bfloat16),
        block_pair[1],
        preferred_element_type=jnp.float32,
    )
    summed = summed * factor[:, :, None] + product
    return (new_best, total, summed)


def attend(video_heads, text_heads):
    heads = video_heads.shape[3]
    width = video_heads.shape[4]
    rows_video = video_heads.shape[1]
    rows_text = text_heads.shape[1]
    joined = jnp.concatenate((video_heads, text_heads), axis=1)
    rows_all = rows_video + rows_text
    joined = joined.reshape(3, rows_all, heads, width)
    queries = joined[0]
    key_pairs = joined[1:]
    initial = (
        jnp.full((heads, rows_all), -jnp.inf, jnp.float32),
        jnp.zeros((heads, rows_all), jnp.float32),
        jnp.zeros((heads, rows_all, width), jnp.float32),
    )
    piece = lax.all_gather(key_pairs, "blk", axis=1, tiled=True)
    count = piece.shape[1] // rows_all

    def one_block(index, inner):
        block_pair = lax.dynamic_slice_in_dim(piece, index * rows_all, rows_all, 1)
        return merge_block(inner, queries, block_pair)

    best, total, summed = lax.fori_loop(0, count, one_block, initial)
    attended = (summed / total[:, :, None]).transpose(1, 0, 2).astype(jnp.bfloat16)
    video_att = attended[:rows_video].reshape(rows_video, 1, heads, width)
    text_att = attended[rows_video:].reshape(rows_text, 1, heads, width)
    return (video_att, text_att)


def on_device(video_qkv, text_qkv, video_gate, text_gate):
    groups = lax.axis_size("uly")
    local_heads = HEADS // groups
    video_rows = video_qkv.shape[1]
    text_rows = text_qkv.shape[1]
    video_split = video_qkv.reshape(3, video_rows, groups, local_heads, HD)
    text_split = text_qkv.reshape(3, text_rows, groups, local_heads, HD)
    video_heads, text_heads = (
        lax.all_to_all(video_split, "uly", split_axis=2, concat_axis=1, tiled=True),
        lax.all_to_all(text_split, "uly", split_axis=2, concat_axis=1, tiled=True),
    )
    video_att, text_att = attend(video_heads, text_heads)
    video_back, text_back = (
        lax.all_to_all(video_att, "uly", split_axis=0, concat_axis=1, tiled=True),
        lax.all_to_all(text_att, "uly", split_axis=0, concat_axis=1, tiled=True),
    )
    video_flat = video_back.reshape(video_rows, HEADS * HD).astype(jnp.float32)
    text_flat = text_back.reshape(text_rows, HEADS * HD).astype(jnp.float32)
    video_out = (video_flat * video_gate[None, :]).astype(jnp.bfloat16)
    text_out = (text_flat * text_gate[None, :]).astype(jnp.bfloat16)
    return (video_out, text_out)


def solution(mesh):
    in_specs = (
        P(None, ("req", "blk", "uly"), None),
        P(None, ("req", "blk", "uly"), None),
        P("req"),
        P("req"),
    )
    out_specs = (P(("req", "blk", "uly"), None), P(("req", "blk", "uly"), None))
    return jax.shard_map(
        on_device, mesh=mesh, in_specs=in_specs, out_specs=out_specs, check_vma=False
    )
```

profile of v0, /device:TPU:0, one launch (start us, length us, event | category | flops | bytes accessed | tf_op | source)
XLA Modules:
  0.0 148.8 jit_solution(10764639887761051975)
XLA Ops:
  7.2 0.8 reshape.38
  8.0 0.6 copy.22
  8.6 4.2 %all-to-all-start.1 = ((bf16[3,2,4,6,128]{4,1,3,0,2:T(2,128)(2,1)}), bf16[3,2,4,6,128]{4,1,3,0,2:T(2,128)(2,1)S(1)}, u32[]{:S(2)}, u32[]{:S(2)}) async-start(bf16[3,2,4,6,128]{4,1,3,0,2:T(2,128)(2,1)} %copy.22), calls=%async_computation.1 | async-start | bytes 73728 | tf_op jit(solution)/shard_map/all_to_all | solution.py:70
  12.9 2.8 %reshape.37 = bf16[3,64,4,6,128]{4,3,2,1,0:T(8,128)(2,1)S(1)} reshape(bf16[3,64,3072]{2,1,0:T(8,128)(2,1)} %param.6) | data formatting | bytes 2359296 | tf_op jit(solution)/shard_map/reshape | solution.py:66
  15.7 1.5 copy.20
  17.2 0.0 all-to-all-done.1
  17.2 3.5 %all-to-all-start = ((bf16[3,64,4,6,128]{4,1,3,0,2:T(8,128)(2,1)}), bf16[3,64,4,6,128]{4,1,3,0,2:T(8,128)(2,1)S(1)}, u32[]{:S(2)}, u32[]{:S(2)}) async-start(bf16[3,64,4,6,128]{4,1,3,0,2:T(8,128)(2,1)} %copy.20), calls=%async_computation | async-start | bytes 2359296 | tf_op jit(solution)/shard_map/all_to_all | solution.py:69
  20.7 0.0 all-gather.3.cloned.1.call-start
  20.8 15.7 %all-to-all-done = bf16[3,64,4,6,128]{4,1,3,0,2:T(8,128)(2,1)S(1)} async-done(((bf16[3,64,4,6,128]{4,1,3,0,2:T(8,128)(2,1)}), bf16[3,64,4,6,128]{4,1,3,0,2:T(8,128)(2,1)S(1)}, u32[]{:S(2)}, u32[]{:S(2)}) %all-to-all-start) | async-done | bytes 1179680 | tf_op jit(solution)/shard_map/all_to_all | solution.py:69
  36.5 0.1 copy.21
  36.6 1.0 fusion.12
  37.6 0.0 all-gather.3.cloned.1.call-update
  37.7 66.0 %all-gather.3.cloned.1.call-done = bf16[2,1056,1,6,128]{4,1,3,0,2:T(8,128)(2,1)} async-done(((bf16[2,264,1,6,128]{4,1,3,0,2:T(8,128)(2,1)}), bf16[2,1056,1,6,128]{4,1,3,0,2:T(8,128)(2,1)}) %all-gather.3.cloned.1.call-update) | async-done | bytes 3244048 | tf_op jit(solution)/shard_map/all_gather | solution.py:47
  103.7 16.6 %while.18 = (s32[]{:T(128)}, f32[6,264]{1,0:T(8,128)S(1)}, f32[6,264]{1,0:T(8,128)S(1)}, f32[6,264,128]{2,1,0:T(8,128)S(1)}, bf16[2,1056,6,128]{3,1,2,0:T(8,128)...) while((s32[]{:T(128)}, f32[6,264]{1,0:T(8,128)S(1)}, ...), condition=%wide.region_3.0_spmd.clone, body=%wide.region_0.0_spmd.clone.sunk | while | flops 218067712 | bytes 7958215 | solution.py:54
  103.7 1.6 %bitcast_reduce_fusion.2 = (f32[6,264]{1,0:T(8,128)S(1)}, f32[6,264,264]{2,1,0:T(8,128)S(1)}) fusion(bf16[264,6,128]{2,0,1:T(8,128)(2,1)S(1)} %get-tuple-element.223, bf16[2,1056,6,128]{3,1,2,0:T(8,128)(2,1)} %get-tuple-element.222, s32[]{:T(128)S(6)} %select_n.9), kind=kOutput, calls=%fused_computation.1.clone.1 | convolution fusion | flops 107887824 | bytes 2490052 | tf_op jit(solution)/shard_map/while/body/eval_jaxpr/qhd,khd->hqk/dot_general | solution.py:15
  105.3 0.4 fusion.24
  105.8 2.0 %convolution_add_fusion.2 = f32[6,264,128]{2,1,0:T(8,128)S(1)} fusion(f32[6,264,264]{2,1,0:T(8,128)S(1)} %get-tuple-element.193, f32[6,264]{1,0:T(8,128)S(1)} %select_maximum_fusion.2, f32[6,264,128]{2,1,0:T(8,128)S(1)} %get-tuple-element.210, bf16[2,1056,6,128]{3,1,2,0:T(8,128)(2,1)} %get-tuple-element.222, s32[]{:T(128)S(6)} %add.53, ...), kind=kOutput, calls=%fused_computation.5.clone.1 | convolution fusion | flops 108915840 | bytes 3712905 | tf_op jit(solution)/shard_map/while/body/eval_jaxpr/hqk,khd->hqd/dot_general | solution.py:22
  107.8 1.6 %bitcast_reduce_fusion.2 = (f32[6,264]{1,0:T(8,128)S(1)}, f32[6,264,264]{2,1,0:T(8,128)S(1)}) fusion(bf16[264,6,128]{2,0,1:T(8,128)(2,1)S(1)} %get-tuple-element.223, bf16[2,1056,6,128]{3,1,2,0:T(8,128)(2,1)} %get-tuple-element.222, s32[]{:T(128)S(6)} %select_n.9), kind=kOutput, calls=%fused_computation.1.clone.1 | convolution fusion | flops 107887824 | bytes 2490052 | tf_op jit(solution)/shard_map/while/body/eval_jaxpr/qhd,khd->hqk/dot_general | solution.py:15
  109.5 0.4 fusion.24
  109.9 2.0 %convolution_add_fusion.2 = f32[6,264,128]{2,1,0:T(8,128)S(1)} fusion(f32[6,264,264]{2,1,0:T(8,128)S(1)} %get-tuple-element.193, f32[6,264]{1,0:T(8,128)S(1)} %select_maximum_fusion.2, f32[6,264,128]{2,1,0:T(8,128)S(1)} %get-tuple-element.210, bf16[2,1056,6,128]{3,1,2,0:T(8,128)(2,1)} %get-tuple-element.222, s32[]{:T(128)S(6)} %add.53, ...), kind=kOutput, calls=%fused_computation.5.clone.1 | convolution fusion | flops 108915840 | bytes 3712905 | tf_op jit(solution)/shard_map/while/body/eval_jaxpr/hqk,khd->hqd/dot_general | solution.py:22
  112.0 1.6 %bitcast_reduce_fusion.2 = (f32[6,264]{1,0:T(8,128)S(1)}, f32[6,264,264]{2,1,0:T(8,128)S(1)}) fusion(bf16[264,6,128]{2,0,1:T(8,128)(2,1)S(1)} %get-tuple-element.223, bf16[2,1056,6,128]{3,1,2,0:T(8,128)(2,1)} %get-tuple-element.222, s32[]{:T(128)S(6)} %select_n.9), kind=kOutput, calls=%fused_computation.1.clone.1 | convolution fusion | flops 107887824 | bytes 2490052 | tf_op jit(solution)/shard_map/while/body/eval_jaxpr/qhd,khd->hqk/dot_general | solution.py:15
  113.6 0.4 fusion.24
  114.1 2.0 %convolution_add_fusion.2 = f32[6,264,128]{2,1,0:T(8,128)S(1)} fusion(f32[6,264,264]{2,1,0:T(8,128)S(1)} %get-tuple-element.193, f32[6,264]{1,0:T(8,128)S(1)} %select_maximum_fusion.2, f32[6,264,128]{2,1,0:T(8,128)S(1)} %get-tuple-element.210, bf16[2,1056,6,128]{3,1,2,0:T(8,128)(2,1)} %get-tuple-element.222, s32[]{:T(128)S(6)} %add.53, ...), kind=kOutput, calls=%fused_computation.5.clone.1 | convolution fusion | flops 108915840 | bytes 3712905 | tf_op jit(solution)/shard_map/while/body/eval_jaxpr/hqk,khd->hqd/dot_general | solution.py:22
  116.2 1.6 %bitcast_reduce_fusion.2 = (f32[6,264]{1,0:T(8,128)S(1)}, f32[6,264,264]{2,1,0:T(8,128)S(1)}) fusion(bf16[264,6,128]{2,0,1:T(8,128)(2,1)S(1)} %get-tuple-element.223, bf16[2,1056,6,128]{3,1,2,0:T(8,128)(2,1)} %get-tuple-element.222, s32[]{:T(128)S(6)} %select_n.9), kind=kOutput, calls=%fused_computation.1.clone.1 | convolution fusion | flops 107887824 | bytes 2490052 | tf_op jit(solution)/shard_map/while/body/eval_jaxpr/qhd,khd->hqk/dot_general | solution.py:15
  117.8 0.4 fusion.24
  118.3 2.0 %convolution_add_fusion.2 = f32[6,264,128]{2,1,0:T(8,128)S(1)} fusion(f32[6,264,264]{2,1,0:T(8,128)S(1)} %get-tuple-element.193, f32[6,264]{1,0:T(8,128)S(1)} %select_maximum_fusion.2, f32[6,264,128]{2,1,0:T(8,128)S(1)} %get-tuple-element.210, bf16[2,1056,6,128]{3,1,2,0:T(8,128)(2,1)} %get-tuple-element.222, s32[]{:T(128)S(6)} %add.53, ...), kind=kOutput, calls=%fused_computation.5.clone.1 | convolution fusion | flops 108915840 | bytes 3712905 | tf_op jit(solution)/shard_map/while/body/eval_jaxpr/hqk,khd->hqd/dot_general | solution.py:22
  120.3 0.0 copy-start.1
  120.3 0.1 copy.24
  120.5 0.4 fusion.13
  120.8 0.6 slice_bitcast_fusion.1
  121.4 3.3 %all-to-all-start.3 = ((bf16[8,1,6,128]{3,2,1,0:T(8,128)(2,1)}), bf16[8,1,6,128]{3,2,1,0:T(8,128)(2,1)S(1)}, u32[]{:S(2)}, u32[]{:S(2)}) async-start(bf16[8,1,6,128]{3,2,1,0:T(8,128)(2,1)} %slice_bitcast_fusion.1), calls=%async_computation.3 | async-start | bytes 32768 | tf_op jit(solution)/shard_map/all_to_all | solution.py:75
  124.7 0.8 slice_bitcast_fusion
  125.5 0.0 copy-start
  125.5 3.0 %all-to-all-done.3 = bf16[8,1,6,128]{3,2,1,0:T(8,128)(2,1)S(1)} async-done(((bf16[8,1,6,128]{3,2,1,0:T(8,128)(2,1)}), bf16[8,1,6,128]{3,2,1,0:T(8,128)(2,1)S(1)}, u32[]{:S(2)}, u32[]{:S(2)}) %all-to-all-start.3) | async-done | bytes 12320 | tf_op jit(solution)/shard_map/all_to_all | solution.py:75
  128.5 3.5 %all-to-all-start.2 = ((bf16[256,1,6,128]{3,2,1,0:T(8,128)(2,1)}), bf16[256,1,6,128]{3,2,1,0:T(8,128)(2,1)S(1)}, u32[]{:S(2)}, u32[]{:S(2)}) async-start(bf16[256,1,6,128]{3,2,1,0:T(8,128)(2,1)} %slice_bitcast_fusion), calls=%async_computation.2 | async-start | bytes 1048576 | tf_op jit(solution)/shard_map/all_to_all | solution.py:74
  132.0 0.0 copy-done.1
  132.0 0.6 multiply_convert_fusion.1
  132.7 8.1 %all-to-all-done.2 = bf16[256,1,6,128]{3,2,1,0:T(8,128)(2,1)S(1)} async-done(((bf16[256,1,6,128]{3,2,1,0:T(8,128)(2,1)}), bf16[256,1,6,128]{3,2,1,0:T(8,128)(2,1)S(1)}, u32[]{:S(2)}, u32[]{:S(2)}) %all-to-all-start.2) | async-done | bytes 393248 | tf_op jit(solution)/shard_map/all_to_all | solution.py:74
  140.8 0.1 copy_bitcast_fusion
  140.9 0.2 reshape.41
  141.1 0.0 copy-done
  141.1 0.8 multiply_convert_fusion
  (19 shorter events, 0.2 us)
Async XLA Ops:
  8.6 8.6 %all-to-all-start.1 = ((bf16[3,2,4,6,128]{4,1,3,0,2:T(2,128)(2,1)}), bf16[3,2,4,6,128]{4,1,3,0,2:T(2,128)(2,1)S(1)}, u32[]{:S(2)}, u32[]{:S(2)}) async-start(bf16[3,2,4,6,128]{4,1,3,0,2:T(2,128)(2,1)} %copy.22), calls=%async_computation.1 | async-start | bytes 73728 | tf_op jit(solution)/shard_map/all_to_all | solution.py:70
  17.2 19.3 %all-to-all-start = ((bf16[3,64,4,6,128]{4,1,3,0,2:T(8,128)(2,1)}), bf16[3,64,4,6,128]{4,1,3,0,2:T(8,128)(2,1)S(1)}, u32[]{:S(2)}, u32[]{:S(2)}) async-start(bf16[3,64,4,6,128]{4,1,3,0,2:T(8,128)(2,1)} %copy.20), calls=%async_computation | async-start | bytes 2359296 | tf_op jit(solution)/shard_map/all_to_all | solution.py:69
  20.7 83.0 %all-gather.3.cloned.1.call-start = ((), (), s32[]{:S(2)}) async-start(), calls=%async_computation.4 | async-start | bytes 4055040 | tf_op jit(solution)/shard_map/all_gather | solution.py:47
  120.3 11.7 %copy-start.1 = (f32[3072]{0:T(1024)S(1)}, f32[3072]{0:T(1024)}, u32[]{:S(2)}) copy-start(f32[3072]{0:T(1024)} %param.9) | copy-start | bytes 36868
  121.4 7.1 %all-to-all-start.3 = ((bf16[8,1,6,128]{3,2,1,0:T(8,128)(2,1)}), bf16[8,1,6,128]{3,2,1,0:T(8,128)(2,1)S(1)}, u32[]{:S(2)}, u32[]{:S(2)}) async-start(bf16[8,1,6,128]{3,2,1,0:T(8,128)(2,1)} %slice_bitcast_fusion.1), calls=%async_computation.3 | async-start | bytes 32768 | tf_op jit(solution)/shard_map/all_to_all | solution.py:75
  125.5 15.6 %copy-start = (f32[3072]{0:T(1024)S(1)}, f32[3072]{0:T(1024)}, u32[]{:S(2)}) copy-start(f32[3072]{0:T(1024)} %param.8) | copy-start | bytes 36868
  128.5 12.3 %all-to-all-start.2 = ((bf16[256,1,6,128]{3,2,1,0:T(8,128)(2,1)}), bf16[256,1,6,128]{3,2,1,0:T(8,128)(2,1)S(1)}, u32[]{:S(2)}, u32[]{:S(2)}) async-start(bf16[256,1,6,128]{3,2,1,0:T(8,128)(2,1)} %slice_bitcast_fusion), calls=%async_computation.2 | async-start | bytes 1048576 | tf_op jit(solution)/shard_map/all_to_all | solution.py:74
Sparse Core Ops, SparseCore 0:
  37.7 65.8 all-gather.2
where the time goes:
time: 150 us; the launch traced here: 149 us
  waiting for transfers between devices  92.8 us (62%)
  starting transfers between devices  14.5 us (10%)
  matrix products  14.5 us (10%)
  between operations  14.2 us (9%)
  local copies, waits for them, and re-layouts  7.71 us (5%)
  other arithmetic  4.76 us (3%)
    all_gather x1, waiting for transfers between devices, attend(): piece = lax.all_gather(key_pairs, 'blk', axis=1, tiled=True)  66 us
    all_to_all x1, waiting for transfers between devices, on_device(): lax.all_to_all(video_split, 'uly', split_axis=2, concat_axis=1, tiled=True)  15.7 us
    all_to_all x1, waiting for transfers between devices, on_device(): lax.all_to_all(video_att, 'uly', split_axis=0, concat_axis=1, tiled=True)  8.12 us
    dot_general x4, matrix products, merge_block(): jnp.einsum('hqk,khd->hqd', raised.astype(jnp.bfloat16), block_pair[1], pr...  8.08 us
    dot_general x4, matrix products, merge_block(): jnp.einsum('qhd,khd->hqk', queries, block_pair[0], preferred_element_type...  6.46 us
    reshape x2, local copies, waits for them, and re-layouts, on_device(): video_split = video_qkv.reshape(3, video_rows, groups, local_heads, HD)  4.32 us
    all_to_all x1, starting transfers between devices, on_device(): lax.all_to_all(text_split, 'uly', split_axis=2, concat_axis=1, tiled=True)  4.24 us
    all_to_all x1, starting transfers between devices, on_device(): lax.all_to_all(video_split, 'uly', split_axis=2, concat_axis=1, tiled=True)  3.53 us
  transfers between devices with their start and end apart: 5, of which 4 were waited for; matrix products, arithmetic and copies ran while one was open for 4% of the time, Pallas kernels for 0%

commit v1 on v0

--- a/solution.py
+++ b/solution.py
@@ -70,8 +70,14 @@
         lax.all_to_all(text_split, "uly", split_axis=2, concat_axis=1, tiled=True),
     )
     video_att, text_att = attend(video_heads, text_heads)
+
+    def lift_roots_on_mesh(sample):
+        new = jnp.stack(jnp.split(sample, lax.axis_size("uly"), axis=0), axis=0)
+        wide_out = lax.all_to_all(new, axis_name="uly", split_axis=0, concat_axis=0)
+        return jnp.concatenate(wide_out, axis=1)
+
     video_back, text_back = (
-        lax.all_to_all(video_att, "uly", split_axis=0, concat_axis=1, tiled=True),
+        lift_roots_on_mesh(video_att),
         lax.all_to_all(text_att, "uly", split_axis=0, concat_axis=1, tiled=True),
     )
     video_flat = video_back.reshape(video_rows, HEADS * HD).astype(jnp.float32)

time: 150 us -> 148 us (0.987)
  no operation moved by 1% of the time
where the time goes in v1:
time: 148 us
  waiting for transfers between devices  91.5 us (62%)
  starting transfers between devices  14.5 us (10%)
  matrix products  14.5 us (10%)
  between operations  14.2 us (10%)
  local copies, waits for them, and re-layouts  7.25 us (5%)
  other arithmetic  5.45 us (4%)
    all_gather x1, waiting for transfers between devices, attend(): piece = lax.all_gather(key_pairs, 'blk', axis=1, tiled=True)  66 us
    all_to_all x1, waiting for transfers between devices, on_device(): lax.all_to_all(video_split, 'uly', split_axis=2, concat_axis=1, tiled=True)  15.7 us
    dot_general x4, matrix products, merge_block(): jnp.einsum('hqk,khd->hqd', raised.astype(jnp.bfloat16), block_pair[1], pr...  8.08 us
    all_to_all x1, waiting for transfers between devices, lift_roots_on_mesh(): wide_out = lax.all_to_all(new, axis_name='uly', split_axis=0, concat_axis=0)  6.71 us
    dot_general x4, matrix products, merge_block(): jnp.einsum('qhd,khd->hqk', queries, block_pair[0], preferred_element_type...  6.46 us
    reshape x2, local copies, waits for them, and re-layouts, on_device(): video_split = video_qkv.reshape(3, video_rows, groups, local_heads, HD)  4.32 us
    all_to_all x1, starting transfers between devices, on_device(): lax.all_to_all(text_split, 'uly', split_axis=2, concat_axis=1, tiled=True)  4.24 us
    all_to_all x1, starting transfers between devices, on_device(): lax.all_to_all(video_split, 'uly', split_axis=2, concat_axis=1, tiled=True)  3.53 us
  transfers between devices with their start and end apart: 5, of which 4 were waited for; matrix products, arithmetic and copies ran while one was open for 4% of the time, Pallas kernels for 0%

profile of v1, /device:TPU:0, one launch (start us, length us, event | category | flops | bytes accessed | tf_op | source)
XLA Modules:
  0.0 147.6 jit_solution(3872706208251128937)
XLA Ops:
  7.2 0.8 reshape.41
  8.0 0.6 copy.31
  8.6 4.2 %all-to-all-start.1 = ((bf16[3,2,4,6,128]{4,1,3,0,2:T(2,128)(2,1)}), bf16[3,2,4,6,128]{4,1,3,0,2:T(2,128)(2,1)S(1)}, u32[]{:S(2)}, u32[]{:S(2)}) async-start(bf16[3,2,4,6,128]{4,1,3,0,2:T(2,128)(2,1)} %copy.31), calls=%async_computation.1 | async-start | bytes 73728 | tf_op jit(solution)/shard_map/all_to_all | solution.py:70
  12.9 2.8 %reshape.40 = bf16[3,64,4,6,128]{4,3,2,1,0:T(8,128)(2,1)S(1)} reshape(bf16[3,64,3072]{2,1,0:T(8,128)(2,1)} %param.6) | data formatting | bytes 2359296 | tf_op jit(solution)/shard_map/reshape | solution.py:66
  15.7 1.5 %copy.29 = bf16[3,64,4,6,128]{4,1,3,0,2:T(8,128)(2,1)} copy(bf16[3,64,4,6,128]{4,3,2,1,0:T(8,128)(2,1)S(1)} %reshape.40) | data formatting | bytes 2359296 | tf_op jit(solution)/shard_map/reshape | solution.py:66
  17.2 0.0 all-to-all-done.1
  17.2 3.5 %all-to-all-start = ((bf16[3,64,4,6,128]{4,1,3,0,2:T(8,128)(2,1)}), bf16[3,64,4,6,128]{4,1,3,0,2:T(8,128)(2,1)S(1)}, u32[]{:S(2)}, u32[]{:S(2)}) async-start(bf16[3,64,4,6,128]{4,1,3,0,2:T(8,128)(2,1)} %copy.29), calls=%async_computation | async-start | bytes 2359296 | tf_op jit(solution)/shard_map/all_to_all | solution.py:69
  20.7 0.0 all-gather.3.cloned.1.call-start
  20.8 15.7 %all-to-all-done = bf16[3,64,4,6,128]{4,1,3,0,2:T(8,128)(2,1)S(1)} async-done(((bf16[3,64,4,6,128]{4,1,3,0,2:T(8,128)(2,1)}), bf16[3,64,4,6,128]{4,1,3,0,2:T(8,128)(2,1)S(1)}, u32[]{:S(2)}, u32[]{:S(2)}) %all-to-all-start) | async-done | bytes 1179680 | tf_op jit(solution)/shard_map/all_to_all | solution.py:69
  36.5 0.1 copy.30
  36.6 1.0 fusion.11
  37.6 0.0 all-gather.3.cloned.1.call-update
  37.7 66.0 %all-gather.3.cloned.1.call-done = bf16[2,1056,1,6,128]{4,1,3,0,2:T(8,128)(2,1)} async-done(((bf16[2,264,1,6,128]{4,1,3,0,2:T(8,128)(2,1)}), bf16[2,1056,1,6,128]{4,1,3,0,2:T(8,128)(2,1)}) %all-gather.3.cloned.1.call-update) | async-done | bytes 3244048 | tf_op jit(solution)/shard_map/all_gather | solution.py:47
  103.7 16.6 %while.18 = (s32[]{:T(128)}, f32[6,264]{1,0:T(8,128)S(1)}, f32[6,264]{1,0:T(8,128)S(1)}, f32[6,264,128]{2,1,0:T(8,128)S(1)}, bf16[2,1056,6,128]{3,1,2,0:T(8,128)...) while((s32[]{:T(128)}, f32[6,264]{1,0:T(8,128)S(1)}, ...), condition=%wide.region_3.0_spmd.clone, body=%wide.region_0.0_spmd.clone.sunk | while | flops 218067712 | bytes 7958215 | solution.py:54
  103.7 1.6 %bitcast_reduce_fusion.2 = (f32[6,264]{1,0:T(8,128)S(1)}, f32[6,264,264]{2,1,0:T(8,128)S(1)}) fusion(bf16[264,6,128]{2,0,1:T(8,128)(2,1)S(1)} %get-tuple-element.227, bf16[2,1056,6,128]{3,1,2,0:T(8,128)(2,1)} %get-tuple-element.226, s32[]{:T(128)S(6)} %select_n.9), kind=kOutput, calls=%fused_computation.1.clone.1 | convolution fusion | flops 107887824 | bytes 2490052 | tf_op jit(solution)/shard_map/while/body/eval_jaxpr/qhd,khd->hqk/dot_general | solution.py:15
  105.3 0.4 fusion.22
  105.8 2.0 %convolution_add_fusion.2 = f32[6,264,128]{2,1,0:T(8,128)S(1)} fusion(f32[6,264,264]{2,1,0:T(8,128)S(1)} %get-tuple-element.197, f32[6,264]{1,0:T(8,128)S(1)} %select_maximum_fusion.2, f32[6,264,128]{2,1,0:T(8,128)S(1)} %get-tuple-element.214, bf16[2,1056,6,128]{3,1,2,0:T(8,128)(2,1)} %get-tuple-element.226, s32[]{:T(128)S(6)} %add.53, ...), kind=kOutput, calls=%fused_computation.5.clone.1 | convolution fusion | flops 108915840 | bytes 3712905 | tf_op jit(solution)/shard_map/while/body/eval_jaxpr/hqk,khd->hqd/dot_general | solution.py:22
  107.9 1.6 %bitcast_reduce_fusion.2 = (f32[6,264]{1,0:T(8,128)S(1)}, f32[6,264,264]{2,1,0:T(8,128)S(1)}) fusion(bf16[264,6,128]{2,0,1:T(8,128)(2,1)S(1)} %get-tuple-element.227, bf16[2,1056,6,128]{3,1,2,0:T(8,128)(2,1)} %get-tuple-element.226, s32[]{:T(128)S(6)} %select_n.9), kind=kOutput, calls=%fused_computation.1.clone.1 | convolution fusion | flops 107887824 | bytes 2490052 | tf_op jit(solution)/shard_map/while/body/eval_jaxpr/qhd,khd->hqk/dot_general | solution.py:15
  109.5 0.4 fusion.22
  110.0 2.0 %convolution_add_fusion.2 = f32[6,264,128]{2,1,0:T(8,128)S(1)} fusion(f32[6,264,264]{2,1,0:T(8,128)S(1)} %get-tuple-element.197, f32[6,264]{1,0:T(8,128)S(1)} %select_maximum_fusion.2, f32[6,264,128]{2,1,0:T(8,128)S(1)} %get-tuple-element.214, bf16[2,1056,6,128]{3,1,2,0:T(8,128)(2,1)} %get-tuple-element.226, s32[]{:T(128)S(6)} %add.53, ...), kind=kOutput, calls=%fused_computation.5.clone.1 | convolution fusion | flops 108915840 | bytes 3712905 | tf_op jit(solution)/shard_map/while/body/eval_jaxpr/hqk,khd->hqd/dot_general | solution.py:22
  112.0 1.6 %bitcast_reduce_fusion.2 = (f32[6,264]{1,0:T(8,128)S(1)}, f32[6,264,264]{2,1,0:T(8,128)S(1)}) fusion(bf16[264,6,128]{2,0,1:T(8,128)(2,1)S(1)} %get-tuple-element.227, bf16[2,1056,6,128]{3,1,2,0:T(8,128)(2,1)} %get-tuple-element.226, s32[]{:T(128)S(6)} %select_n.9), kind=kOutput, calls=%fused_computation.1.clone.1 | convolution fusion | flops 107887824 | bytes 2490052 | tf_op jit(solution)/shard_map/while/body/eval_jaxpr/qhd,khd->hqk/dot_general | solution.py:15
  113.6 0.4 fusion.22
  114.1 2.0 %convolution_add_fusion.2 = f32[6,264,128]{2,1,0:T(8,128)S(1)} fusion(f32[6,264,264]{2,1,0:T(8,128)S(1)} %get-tuple-element.197, f32[6,264]{1,0:T(8,128)S(1)} %select_maximum_fusion.2, f32[6,264,128]{2,1,0:T(8,128)S(1)} %get-tuple-element.214, bf16[2,1056,6,128]{3,1,2,0:T(8,128)(2,1)} %get-tuple-element.226, s32[]{:T(128)S(6)} %add.53, ...), kind=kOutput, calls=%fused_computation.5.clone.1 | convolution fusion | flops 108915840 | bytes 3712905 | tf_op jit(solution)/shard_map/while/body/eval_jaxpr/hqk,khd->hqd/dot_general | solution.py:22
  116.2 1.6 %bitcast_reduce_fusion.2 = (f32[6,264]{1,0:T(8,128)S(1)}, f32[6,264,264]{2,1,0:T(8,128)S(1)}) fusion(bf16[264,6,128]{2,0,1:T(8,128)(2,1)S(1)} %get-tuple-element.227, bf16[2,1056,6,128]{3,1,2,0:T(8,128)(2,1)} %get-tuple-element.226, s32[]{:T(128)S(6)} %select_n.9), kind=kOutput, calls=%fused_computation.1.clone.1 | convolution fusion | flops 107887824 | bytes 2490052 | tf_op jit(solution)/shard_map/while/body/eval_jaxpr/qhd,khd->hqk/dot_general | solution.py:15
  117.8 0.4 fusion.22
  118.3 2.0 %convolution_add_fusion.2 = f32[6,264,128]{2,1,0:T(8,128)S(1)} fusion(f32[6,264,264]{2,1,0:T(8,128)S(1)} %get-tuple-element.197, f32[6,264]{1,0:T(8,128)S(1)} %select_maximum_fusion.2, f32[6,264,128]{2,1,0:T(8,128)S(1)} %get-tuple-element.214, bf16[2,1056,6,128]{3,1,2,0:T(8,128)(2,1)} %get-tuple-element.226, s32[]{:T(128)S(6)} %add.53, ...), kind=kOutput, calls=%fused_computation.5.clone.1 | convolution fusion | flops 108915840 | bytes 3712905 | tf_op jit(solution)/shard_map/while/body/eval_jaxpr/hqk,khd->hqd/dot_general | solution.py:22
  120.3 0.0 copy-start.1
  120.3 0.3 fusion.13
  120.7 0.6 copy.34
  121.3 3.2 %all-to-all-start.3 = ((bf16[8,1,6,128]{3,2,1,0:T(8,128)(2,1)}), bf16[8,1,6,128]{3,2,1,0:T(8,128)(2,1)S(1)}, u32[]{:S(2)}, u32[]{:S(2)}) async-start(bf16[8,1,6,128]{3,2,1,0:T(8,128)(2,1)} %copy.34), calls=%async_computation.3 | async-start | bytes 32768 | tf_op jit(solution)/shard_map/all_to_all | solution.py:81
  124.5 0.8 pad_maximum_fusion.1
  125.3 3.0 %all-to-all-done.3 = bf16[8,1,6,128]{3,2,1,0:T(8,128)(2,1)S(1)} async-done(((bf16[8,1,6,128]{3,2,1,0:T(8,128)(2,1)}), bf16[8,1,6,128]{3,2,1,0:T(8,128)(2,1)S(1)}, u32[]{:S(2)}, u32[]{:S(2)}) %all-to-all-start.3) | async-done | bytes 12320 | tf_op jit(solution)/shard_map/all_to_all | solution.py:81
  128.3 3.5 %all-to-all-start.2 = ((bf16[4,64,1,6,128]{4,1,3,2,0:T(8,128)(2,1)}), bf16[4,64,1,6,128]{4,1,3,2,0:T(8,128)(2,1)S(1)}, u32[]{:S(2)}, u32[]{:S(2)}) async-start(bf16[4,64,1,6,128]{4,1,3,2,0:T(8,128)(2,1)} %pad_maximum_fusion.1), calls=%async_computation.2 | async-start | bytes 786432 | tf_op jit(solution)/shard_map/all_to_all | solution.py:76
  131.9 0.0 copy-done.1
  131.9 0.6 multiply_convert_fusion.1
  132.5 0.0 copy-start
  132.5 6.7 %all-to-all-done.2 = bf16[4,64,1,6,128]{4,1,3,2,0:T(8,128)(2,1)S(1)} async-done(((bf16[4,64,1,6,128]{4,1,3,2,0:T(8,128)(2,1)}), bf16[4,64,1,6,128]{4,1,3,2,0:T(8,128)(2,1)S(1)}, u32[]{:S(2)}, u32[]{:S(2)}) %all-to-all-start.2) | async-done | bytes 393248 | tf_op jit(solution)/shard_map/all_to_all | solution.py:76
  139.2 0.1 convert_bitcast_fusion
  139.3 0.5 copy.33
  139.8 0.2 reshape.43
  139.9 0.0 copy-done
  140.0 0.8 multiply_convert_fusion
  (21 shorter events, 0.2 us)
Async XLA Ops:
  8.6 8.6 %all-to-all-start.1 = ((bf16[3,2,4,6,128]{4,1,3,0,2:T(2,128)(2,1)}), bf16[3,2,4,6,128]{4,1,3,0,2:T(2,128)(2,1)S(1)}, u32[]{:S(2)}, u32[]{:S(2)}) async-start(bf16[3,2,4,6,128]{4,1,3,0,2:T(2,128)(2,1)} %copy.31), calls=%async_computation.1 | async-start | bytes 73728 | tf_op jit(solution)/shard_map/all_to_all | solution.py:70
  17.2 19.3 %all-to-all-start = ((bf16[3,64,4,6,128]{4,1,3,0,2:T(8,128)(2,1)}), bf16[3,64,4,6,128]{4,1,3,0,2:T(8,128)(2,1)S(1)}, u32[]{:S(2)}, u32[]{:S(2)}) async-start(bf16[3,64,4,6,128]{4,1,3,0,2:T(8,128)(2,1)} %copy.29), calls=%async_computation | async-start | bytes 2359296 | tf_op jit(solution)/shard_map/all_to_all | solution.py:69
  20.7 83.0 %all-gather.3.cloned.1.call-start = ((), (), s32[]{:S(2)}) async-start(), calls=%async_computation.4 | async-start | bytes 4055040 | tf_op jit(solution)/shard_map/all_gather | solution.py:47
  120.3 11.5 %copy-start.1 = (f32[3072]{0:T(1024)S(1)}, f32[3072]{0:T(1024)}, u32[]{:S(2)}) copy-start(f32[3072]{0:T(1024)} %param.9) | copy-start | bytes 36868
  121.3 7.1 %all-to-all-start.3 = ((bf16[8,1,6,128]{3,2,1,0:T(8,128)(2,1)}), bf16[8,1,6,128]{3,2,1,0:T(8,128)(2,1)S(1)}, u32[]{:S(2)}, u32[]{:S(2)}) async-start(bf16[8,1,6,128]{3,2,1,0:T(8,128)(2,1)} %copy.34), calls=%async_computation.3 | async-start | bytes 32768 | tf_op jit(solution)/shard_map/all_to_all | solution.py:81
  128.3 10.8 %all-to-all-start.2 = ((bf16[4,64,1,6,128]{4,1,3,2,0:T(8,128)(2,1)}), bf16[4,64,1,6,128]{4,1,3,2,0:T(8,128)(2,1)S(1)}, u32[]{:S(2)}, u32[]{:S(2)}) async-start(bf16[4,64,1,6,128]{4,1,3,2,0:T(8,128)(2,1)} %pad_maximum_fusion.1), calls=%async_computation.2 | async-start | bytes 786432 | tf_op jit(solution)/shard_map/all_to_all | solution.py:76
  132.5 7.5 %copy-start = (f32[3072]{0:T(1024)S(1)}, f32[3072]{0:T(1024)}, u32[]{:S(2)}) copy-start(f32[3072]{0:T(1024)} %param.8) | copy-start | bytes 36868
Sparse Core Ops, SparseCore 0:
  37.8 65.8 all-gather.2
